TPU v7x, 32 devices: a 4x4x1 block of a 4x4x8 slice. The times are simulated.
32 devices in a mesh: rep: 2 (over z, core), dp: 16 (over x, y).
Axes of the slice: x: 4, y: 4, z: 1, core: 2. Of those that a mesh axis runs over, the one named last changes fastest.
The devices are a block of a 4x4x8 slice.
Arguments:
- x: bfloat16 [32, 2048, 768], P(('rep', 'dp')), parts along dimension 0
- dy: bfloat16 [32, 2048, 768], P(('rep', 'dp')), parts along dimension 0
- w_gate: bfloat16 [2, 768, 1792], replicated
- w_up: bfloat16 [2, 768, 1792], replicated
- w_down: bfloat16 [2, 1792, 768], replicated
- m_w_gate: float32 [2, 768, 1792], P(None, 'dp')
- m_w_up: float32 [2, 768, 1792], P(None, 'dp')
- m_w_down: float32 [2, 1792, 768], P(None, 'dp')
- v_w_gate: float32 [2, 768, 1792], P(None, 'dp')
- v_w_up: float32 [2, 768, 1792], P(None, 'dp')
- v_w_down: float32 [2, 1792, 768], P(None, 'dp')
Outputs:
- output 1: bfloat16 [4, 768, 1792], P('rep'), parts along dimension 0
- output 2: bfloat16 [4, 768, 1792], P('rep'), parts along dimension 0
- output 3: bfloat16 [4, 1792, 768], P('rep'), parts along dimension 0
- output 4: float32 [4, 768, 1792], P('rep', 'dp'), parts along dimension 0
- output 5: float32 [4, 768, 1792], P('rep', 'dp'), parts along dimension 0
- output 6: float32 [4, 1792, 768], P('rep', 'dp'), parts along dimension 0
- output 7: float32 [4, 768, 1792], P('rep', 'dp'), parts along dimension 0
- output 8: float32 [4, 768, 1792], P('rep', 'dp'), parts along dimension 0
- output 9: float32 [4, 1792, 768], P('rep', 'dp'), parts along dimension 0
There are 2 independent parts. A program takes and returns all parts, laid end to end along the dimension named above; an argument that names none is the same for every part.
All inputs are finite; a program needn't handle non-finite values.
Results may differ from a plain program's by a relative error of at most 0.022.
Values are sent between devices in bfloat16 or wider.
A program may use at most 768 MiB of HBM per device.

v0:
```python
import jax
import jax.numpy as jnp
from jax import lax

NAMES = ("w_gate", "w_up", "w_down")


def matmul(a, w):
    return jnp.dot(a, w, preferred_element_type=jnp.float32).astype(jnp.bfloat16)


def normed(h):
    wide = h.astype(jnp.float32)
    scale = lax.rsqrt(jnp.mean(wide**2, -1, keepdims=True) + 1e-6)
    return (wide * scale).astype(jnp.bfloat16)


def layer(h, w):
    a = normed(h)
    gate = jnp.dot(a, w["w_gate"], preferred_element_type=jnp.float32)
    up = jnp.dot(a, w["w_up"], preferred_element_type=jnp.float32)
    return h + matmul((jax.nn.silu(gate) * up).astype(jnp.bfloat16), w["w_down"])


def adamw(w, m, v, g):
    m = 0.9 * m + 0.1 * g
    v = 0.95 * v + 0.05 * g * g
    step = m * lax.rsqrt(v + 1e-8) + 0.1 * w
    return (w - 0.02 * step).astype(jnp.bfloat16), m, v


def clipped(gradients, sum_of_squares, count):
    factor = jnp.minimum(1.0, 0.5 * lax.rsqrt(sum_of_squares / count + 1e-30))
    return [g * factor for g in gradients]


def stack(weights, h):
    for number in range(weights["w_gate"].shape[0]):
        h = layer(h, {name: w[number] for name, w in weights.items()})
    return h


def solution(mesh):
    groups = mesh.shape["rep"]

    def step(x, dy, *arrays):
        weights, m, v = (arrays[i : i + 3] for i in (0, 3, 6))
        x, dy = (t.reshape(groups, -1, *t.shape[1:]) for t in (x, dy))

        def of_a_group(x, dy):
            _, back = jax.vjp(lambda w: stack(w, x), dict(zip(NAMES, weights, strict=True)))
            by_weights = back(dy)[0]
            gradients = [by_weights[name].astype(jnp.float32) for name in NAMES]
            gradients = clipped(gradients, sum(jnp.sum(g * g) for g in gradients), sum(g.size for g in gradients))
            new = [adamw(w.astype(jnp.float32), m, v, g) for w, m, v, g in zip(weights, m, v, gradients, strict=True)]
            return tuple(one[which] for which in range(3) for one in new)

        return tuple(t.reshape(-1, *t.shape[2:]) for t in jax.vmap(of_a_group)(x, dy))

    return step
```

profile of v0, /device:TPU:97, one launch (start us, length us, event | category | flops | bytes accessed | tf_op | source)
XLA Modules:
  0.0 830.7 jit_solution(9508502820357509817)
XLA Ops:
  7.2 0.1 reduce-scatter.29.cloned.1.call-start
  7.3 2.7 fusion.35
  10.0 4.6 copy
  14.7 7.8 fusion.77
  22.5 13.2 %fusion.75 = f32[2048,1792]{1,0:T(8,128)S(1)} fusion(bf16[2,768,1792]{2,1,0:T(8,128)(2,1)} %param.3, bf16[1,2048,768]{2,1,0:T(8,128)(2,1)} %param.2, f32[2048]{0:T(1024)S(1)} %add_rsqrt_fusion), kind=kOutput, calls=%fused_computation.86 | convolution fusion | flops 5641863168 | bytes 20586496 | tf_op jit(solution)/vmap(jvp())/dot_general | solution.py:21
  35.7 7.4 fusion.26
  43.2 10.1 %fusion.39 = (f32[2048]{0:T(1024)S(1)}, bf16[1,1,2048,768]{2,3,1,0:T(8,128)(2,1)S(1)}) fusion(bf16[2048,1792]{1,0:T(8,128)(2,1)} %fusion.26, bf16[2,1792,768]{2,1,0:T(8,128)(2,1)} %param.4, bf16[1,2048,768]{1,2,0:T(8,128)(2,1)} %copy), kind=kOutput, calls=%fused_computation.56 | convolution fusion | flops 5645006848 | bytes 16392192 | tf_op jit(solution)/vmap(jvp())/dot_general | solution.py:9
  53.3 12.1 %fusion.66 = f32[2048,1792]{1,0:T(8,128)} fusion(bf16[2,768,1792]{2,1,0:T(8,128)(2,1)} %param, bf16[1,1,2048,768]{2,3,1,0:T(8,128)(2,1)S(1)} %get-tuple-element.10, f32[2048]{0:T(1024)S(1)} %bitcast.355), kind=kOutput, calls=%fused_computation.77 | convolution fusion | flops 5641863168 | bytes 20586496 | tf_op jit(solution)/vmap(jvp())/dot_general | solution.py:20
  65.4 11.0 %fusion.69 = f32[2048,1792]{1,0:T(8,128)} fusion(bf16[2,768,1792]{2,1,0:T(8,128)(2,1)} %param.3, bf16[1,1,2048,768]{2,3,1,0:T(8,128)(2,1)S(1)} %get-tuple-element.10, f32[2048]{0:T(1024)S(1)} %bitcast.356), kind=kOutput, calls=%fused_computation.80 | convolution fusion | flops 5641863168 | bytes 20586496 | tf_op jit(solution)/vmap(jvp())/dot_general | solution.py:21
  76.5 8.5 %convolution_convert_fusion.1 = bf16[2048,1792]{1,0:T(8,128)(2,1)} fusion(bf16[1,2048,768]{2,1,0:T(8,128)(2,1)S(1)} %copy-done.5, bf16[2,1792,768]{2,1,0:T(8,128)(2,1)S(1)} %bitcast.361), kind=kOutput, calls=%fused_computation.43 | convolution fusion | flops 5640814592 | bytes 13238272 | tf_op jit(solution)/vmap(transpose(jvp()))/dot_general | solution.py:9
  84.9 3.2 copy.1
  88.1 13.4 %fusion.6 = bf16[2048,1792]{1,0:T(8,128)(2,1)S(1)} fusion(f32[2048,1792]{1,0:T(8,128)} %fusion.66, f32[2048,1792]{1,0:T(8,128)} %fusion.69, bf16[2048,1792]{1,0:T(8,128)(2,1)} %convolution_convert_fusion.1), kind=kLoop, calls=%fused_computation.11 | loop fusion | flops 44040192 | bytes 44040192
  101.6 2.9 copy-done.3
  104.5 7.6 convolution_convert_fusion.2
  112.2 13.1 %fusion.41 = (f32[2048]{0:T(1024)S(1)}, bf16[2048,768]{0,1:T(8,128)(2,1)}) fusion(bf16[1,1,2048,768]{2,3,1,0:T(8,128)(2,1)S(1)} %copy-done.9, bf16[2048,768]{0,1:T(8,128)(2,1)S(1)} %convolution_convert_fusion.2, bf16[2,768,1792]{2,1,0:T(8,128)(2,1)} %param.3, bf16[2048,1792]{1,0:T(8,128)(2,1)} %convolution_convert_fusion.1, f32[2048,1792]{1,0:T(8,128)} %fusion.66), kind=kOutput, calls=%fused_computation.58 | convolution fusion | flops 5668599808 | bytes 34217984 | tf_op jit(solution)/vmap(transpose(jvp()))/dot_general | solution.py:21
  125.2 4.1 fusion.60
  129.4 1.7 copy-done.10
  131.0 10.1 %convolution_bitcast_fusion = f32[1,1792,768]{2,1,0:T(8,128)} fusion(bf16[2048,1792]{1,0:T(8,128)(2,1)} %fusion.26, bf16[2048,768]{0,1:T(8,128)(2,1)S(1)} %fusion.60), kind=kOutput, calls=%fused_computation.63 | convolution fusion | flops 5637144576 | bytes 15990784 | tf_op jit(solution)/vmap(transpose(jvp()))/dot_general | solution.py:9
  141.1 0.1 reduce-scatter.29.cloned.1.call-update
  141.2 0.1 reduce-scatter.27.cloned.1.call-start
  141.3 14.4 %fusion.42 = f32[1,1792,768]{2,1,0:T(8,128)} fusion(f32[2048,1792]{1,0:T(8,128)} %fusion.69, f32[2048,1792]{1,0:T(8,128)} %fusion.66, bf16[1,2048,768]{2,1,0:T(8,128)(2,1)S(1)} %copy-done.6), kind=kOutput, calls=%fused_computation.60 | convolution fusion | flops 5659164672 | bytes 38010880 | tf_op jit(solution)/vmap(transpose(jvp()))/dot_general | solution.py:9
  155.7 0.1 reduce-scatter.27.cloned.1.call-update
  155.7 0.1 reduce-scatter.25.cloned.1.call-start
  155.8 8.8 %convolution_convert_fusion = bf16[2048,1792]{1,0:T(8,128)(2,1)S(1)} fusion(bf16[2048,768]{0,1:T(8,128)(2,1)} %copy-done.10, bf16[2,1792,768]{2,1,0:T(8,128)(2,1)} %param.4), kind=kOutput, calls=%fused_computation.42 | convolution fusion | flops 5640814592 | bytes 13238272 | tf_op jit(solution)/vmap(transpose(jvp()))/dot_general | solution.py:9
  164.6 3.0 copy-done.17
  167.7 11.9 %fusion.48 = f32[1,768,1792]{2,1,0:T(8,128)} fusion(bf16[2048,1792]{1,0:T(8,128)(2,1)S(1)} %convolution_convert_fusion, f32[2048,1792]{1,0:T(8,128)} %copy-done, bf16[1,2048,768]{1,2,0:T(8,128)(2,1)S(1)} %copy-done.7, f32[2048]{0:T(1024)S(1)} %copy-done.15), kind=kOutput, calls=%fused_computation.62 | convolution fusion | flops 5663883264 | bytes 30679040 | tf_op jit(solution)/vmap(transpose(jvp()))/dot_general | solution.py:21
  179.7 0.1 reduce-scatter.23.cloned.1.call-start
  179.7 13.9 %fusion.45 = f32[1,768,1792]{2,1,0:T(8,128)} fusion(bf16[2048,1792]{1,0:T(8,128)(2,1)} %convolution_convert_fusion.1, f32[2048,1792]{1,0:T(8,128)} %fusion.66, bf16[1,1,2048,768]{2,3,1,0:T(8,128)(2,1)} %copy-done.8, f32[2048]{0:T(1024)S(1)} %bitcast.358), kind=kOutput, calls=%fused_computation.61 | convolution fusion | flops 5663883264 | bytes 30679040 | tf_op jit(solution)/vmap(transpose(jvp()))/dot_general | solution.py:21
  193.6 0.1 reduce-scatter.23.cloned.1.call-update
  193.7 0.1 reduce-scatter.21.cloned.1.call-start
  193.8 17.5 %fusion.51 = f32[1,768,1792]{2,1,0:T(8,128)} fusion(f32[2048,1792]{1,0:T(8,128)} %copy-done, f32[2048,1792]{1,0:T(8,128)} %copy-done.1, bf16[2048,1792]{1,0:T(8,128)(2,1)} %copy-done.17, bf16[1,2048,768]{1,2,0:T(8,128)(2,1)S(1)} %copy-done.7, f32[2048]{0:T(1024)S(1)} %copy-done.15), kind=kOutput, calls=%fused_computation.65 | convolution fusion | flops 5682233344 | bytes 45359104 | tf_op jit(solution)/vmap(transpose(jvp()))/dot_general | solution.py:20
  211.4 0.1 reduce-scatter.19.cloned.1.call-start
  211.4 11.2 %convolution_bitcast_fusion.1 = f32[1,768,1792]{2,1,0:T(8,128)} fusion(bf16[2048,1792]{1,0:T(8,128)(2,1)} %copy-done.3, bf16[1,1,2048,768]{2,3,1,0:T(8,128)(2,1)} %copy-done.8, f32[2048]{0:T(1024)S(1)} %bitcast.359), kind=kOutput, calls=%fused_computation.64 | convolution fusion | flops 5641863168 | bytes 15998976 | tf_op jit(solution)/vmap(transpose(jvp()))/dot_general | solution.py:20
  222.6 0.1 reduce-scatter.19.cloned.1.call-update
  222.7 0.1 all-gather.14.cloned.1.call-start
  222.7 0.6 dynamic-slice
  224.0 1.0 convert_bitcast_fusion.3
  225.0 71.0 %reduce-scatter.27.cloned.1.call-done = f32[1,112,768]{2,1,0:T(8,128)} async-done(((f32[1,1792,768]{2,1,0:T(8,128)}), f32[1,112,768]{2,1,0:T(8,128)}) %reduce-scatter.27.cloned.1.call-update) | async-done | bytes 344080
  296.0 1.0 convert_bitcast_fusion.4
  297.0 0.8 fusion.112
  297.8 76.2 %reduce-scatter.25.cloned.1.call-done = f32[1,48,1792]{2,1,0:T(8,128)} async-done(((f32[1,768,1792]{2,1,0:T(8,128)}), f32[1,48,1792]{2,1,0:T(8,128)}) %reduce-scatter.25.cloned.1.call-update) | async-done | bytes 344080
  374.0 1.0 convert_bitcast_fusion.5
  375.0 76.4 %reduce-scatter.23.cloned.1.call-done = f32[1,48,1792]{2,1,0:T(8,128)} async-done(((f32[1,768,1792]{2,1,0:T(8,128)}), f32[1,48,1792]{2,1,0:T(8,128)}) %reduce-scatter.23.cloned.1.call-update) | async-done | bytes 344080
  451.4 1.0 convert_bitcast_fusion.6
  452.4 0.8 fusion.111
  453.1 76.0 %reduce-scatter.21.cloned.1.call-done = f32[1,48,1792]{2,1,0:T(8,128)} async-done(((f32[1,768,1792]{2,1,0:T(8,128)}), f32[1,48,1792]{2,1,0:T(8,128)}) %reduce-scatter.21.cloned.1.call-update) | async-done | bytes 344080
  529.1 1.0 convert_bitcast_fusion.7
  530.1 77.0 %reduce-scatter.19.cloned.1.call-done = f32[1,48,1792]{2,1,0:T(8,128)} async-done(((f32[1,768,1792]{2,1,0:T(8,128)}), f32[1,48,1792]{2,1,0:T(8,128)}) %reduce-scatter.19.cloned.1.call-update) | async-done | bytes 344080
  607.1 1.0 convert_bitcast_fusion.8
  608.1 0.8 fusion.110
  610.8 32.1 %all-reduce.16 = f32[1]{0:T(128)} all-reduce(f32[1]{0:T(128)} %bitcast.50), channel_id=5, replica_groups=mesh['rep'=2,'dp'=16] {'dp'}, use_global_device_ids=true, to_apply=%region_3.4.clone | all-reduce | flops 1 | bytes 8 | tf_op jit(solution)/vmap()/reduce_sum | solution.py:54
  643.6 2.6 fusion.129
  646.2 0.1 all-gather.12.cloned.1.call-start
  646.3 2.8 fusion.130
  649.2 0.1 all-gather.10.cloned.1.call-start
  649.2 3.0 fusion.131
  652.3 50.8 %all-gather.14.cloned.1.call-done = bf16[1,2,1792,768]{3,2,1,0:T(8,128)(2,1)} async-done(((bf16[1,2,112,768]{3,2,1,0:T(8,128)(2,1)}), bf16[1,2,1792,768]{3,2,1,0:T(8,128)(2,1)}) %all-gather.14.cloned.1.call-update) | async-done | bytes 5505040 | tf_op jit(solution)/reshape | solution.py:58
  703.1 54.2 %all-gather.12.cloned.1.call-done = bf16[1,2,768,1792]{3,2,1,0:T(8,128)(2,1)} async-done(((bf16[1,2,48,1792]{3,2,1,0:T(8,128)(2,1)}), bf16[1,2,768,1792]{3,2,1,0:T(8,128)(2,1)}) %all-gather.12.cloned.1.call-update) | async-done | bytes 5505040 | tf_op jit(solution)/reshape | solution.py:58
  757.2 54.2 %all-gather.10.cloned.1.call-done = bf16[1,2,768,1792]{3,2,1,0:T(8,128)(2,1)} async-done(((bf16[1,2,48,1792]{3,2,1,0:T(8,128)(2,1)}), bf16[1,2,768,1792]{3,2,1,0:T(8,128)(2,1)}) %all-gather.10.cloned.1.call-update) | async-done | bytes 5505040 | tf_op jit(solution)/reshape | solution.py:58
  811.4 5.9 copy.5
  817.3 2.8 copy.6
  820.1 0.1 slice-done
  820.2 1.1 slice-done.1
  821.3 2.4 copy.7
  (51 shorter events, 0.4 us)
Async XLA Ops:
  7.2 7.5 copy-start.2
  7.2 216.8 %reduce-scatter.29.cloned.1.call-start = ((), (), s32[]{:S(2)}) async-start(), calls=%async_computation.14 | async-start | bytes 5849088
  14.6 7.9 copy-start.14
  22.5 13.2 %copy-start = (f32[2048,1792]{1,0:T(8,128)}, f32[2048,1792]{1,0:T(8,128)S(1)}, u32[]{:S(2)}) copy-start(f32[2048,1792]{1,0:T(8,128)S(1)} %fusion.77) | copy-start | bytes 44040196
  35.7 7.4 copy-start.1
  43.1 33.3 %slice-start.2 = ((s8[5505024]{0:T(1024)(128)(4,1)}), s8[4194304]{0:T(1024)(128)(4,1)S(1)}, s32[]{:S(2)}) async-start(s8[5505024]{0:T(1024)(128)(4,1)} %bitcast.360), calls=%async_computation.17 | async-start | bytes 8388608
  53.2 12.2 %copy-start.8 = (bf16[1,1,2048,768]{2,3,1,0:T(8,128)(2,1)}, bf16[1,1,2048,768]{2,3,1,0:T(8,128)(2,1)S(1)}, u32[]{:S(2)}) copy-start(bf16[1,1,2048,768]{2,3,1,0:T(8,128)(2,1)S(1)} %get-tuple-element.10) | copy-start | bytes 9437188
  53.3 23.2 %slice-start.3 = ((s8[5505024]{0:T(1024)(128)(4,1)}), s8[1310720]{0:T(1024)(128)(4,1)S(1)}, s32[]{:S(2)}) async-start(s8[5505024]{0:T(1024)(128)(4,1)} %bitcast.360), calls=%async_computation.18 | async-start | bytes 2621440
  65.4 11.0 %copy-start.5 = (bf16[1,2048,768]{2,1,0:T(8,128)(2,1)S(1)}, bf16[1,2048,768]{2,1,0:T(8,128)(2,1)}, u32[]{:S(2)}) copy-start(bf16[1,2048,768]{2,1,0:T(8,128)(2,1)} %param.5) | copy-start | bytes 9437188
  101.6 3.0 copy-start.3
  104.5 7.6 copy-start.9
  129.3 1.7 copy-start.10
  131.0 10.3 %copy-start.6 = (bf16[1,2048,768]{2,1,0:T(8,128)(2,1)S(1)}, bf16[1,2048,768]{2,1,0:T(8,128)(2,1)}, u32[]{:S(2)}) copy-start(bf16[1,2048,768]{2,1,0:T(8,128)(2,1)} %param.5) | copy-start | bytes 9437188
  141.2 154.8 %reduce-scatter.27.cloned.1.call-start = ((), (), s32[]{:S(2)}) async-start(), calls=%async_computation.13 | async-start | bytes 5849088
  155.7 11.9 %copy-start.7 = (bf16[1,2048,768]{1,2,0:T(8,128)(2,1)S(1)}, bf16[1,2048,768]{1,2,0:T(8,128)(2,1)}, u32[]{:S(2)}) copy-start(bf16[1,2048,768]{1,2,0:T(8,128)(2,1)} %copy) | copy-start | bytes 9437188
  155.7 11.9 %copy-start.15 = (f32[2048]{0:T(1024)S(1)}, f32[2048]{0:T(1024)}, u32[]{:S(2)}) copy-start(f32[2048]{0:T(1024)} %copy-done.14) | copy-start | bytes 24580
  155.7 218.2 %reduce-scatter.25.cloned.1.call-start = ((), (), s32[]{:S(2)}) async-start(), calls=%async_computation.12 | async-start | bytes 5849088
  164.6 3.0 copy-start.17
  179.7 271.7 %reduce-scatter.23.cloned.1.call-start = ((), (), s32[]{:S(2)}) async-start(), calls=%async_computation.11 | async-start | bytes 5849088
  193.7 335.4 %reduce-scatter.21.cloned.1.call-start = ((), (), s32[]{:S(2)}) async-start(), calls=%async_computation.10 | async-start | bytes 5849088
  211.3 11.4 %copy-start.16 = (u32[32]{0:T(128)S(1)}, u32[32]{0:T(128)}, u32[]{:S(2)}) copy-start(u32[32]{0:T(128)} %constant.74) | copy-start | bytes 388
  211.4 395.7 %reduce-scatter.19.cloned.1.call-start = ((), (), s32[]{:S(2)}) async-start(), calls=%async_computation.9 | async-start | bytes 5849088
  222.6 421.0 %copy-start.11 = (f32[2,112,768]{2,1,0:T(8,128)S(1)}, f32[2,112,768]{2,1,0:T(8,128)}, u32[]{:S(2)}) copy-start(f32[2,112,768]{2,1,0:T(8,128)} %param.10) | copy-start | bytes 2064388
  222.6 421.0 %copy-start.12 = (f32[2,112,768]{2,1,0:T(8,128)S(1)}, f32[2,112,768]{2,1,0:T(8,128)}, u32[]{:S(2)}) copy-start(f32[2,112,768]{2,1,0:T(8,128)} %param.9) | copy-start | bytes 2064388
  222.6 423.7 %copy-start.13 = (f32[2,48,1792]{2,1,0:T(8,128)S(1)}, f32[2,48,1792]{2,1,0:T(8,128)}, u32[]{:S(2)}) copy-start(f32[2,48,1792]{2,1,0:T(8,128)} %param.8) | copy-start | bytes 2064388
  222.7 480.4 %all-gather.14.cloned.1.call-start = ((), (), s32[]{:S(2)}) async-start(), calls=%async_computation.8 | async-start | bytes 5849088 | tf_op jit(solution)/reshape | solution.py:58
  646.2 111.0 %all-gather.12.cloned.1.call-start = ((), (), s32[]{:S(2)}) async-start(), calls=%async_computation.7 | async-start | bytes 5849088 | tf_op jit(solution)/reshape | solution.py:58
  649.2 162.2 %all-gather.10.cloned.1.call-start = ((), (), s32[]{:S(2)}) async-start(), calls=%async_computation.6 | async-start | bytes 5849088 | tf_op jit(solution)/reshape | solution.py:58
  811.4 5.9 copy-start.4
  811.4 8.8 %slice-start = ((s8[5505024]{0:T(1024)(128)(4,1)}), s8[4194304]{0:T(1024)(128)(4,1)S(1)}, s32[]{:S(2)}) async-start(s8[5505024]{0:T(1024)(128)(4,1)} %bitcast.347), calls=%async_computation.15 | async-start | bytes 8388608
  817.3 4.0 slice-start.1
Sparse Core Ops, SparseCore 0:
  141.3 77.0 reduce-scatter.28
  221.6 74.3 reduce-scatter.26
  299.8 74.1 reduce-scatter.24
  377.0 74.2 reduce-scatter.22
  455.0 74.0 reduce-scatter.20
  532.8 74.2 reduce-scatter.18
  646.4 56.6 all-gather.13
  705.6 51.5 all-gather.11
  759.8 51.5 all-gather.9
where the time goes:
time: 840 us; the launch traced here: 831 us
  waiting for transfers between devices  536 us (64%)
  matrix products  171 us (20%)
  other arithmetic  44.4 us (5%)
  blocking collectives  32.1 us (4%)
  local copies, waits for them, and re-layouts  28.4 us (3%)
  between operations  17.9 us (2%)
    unnamed x15, waiting for transfers between devices  377 us
    reshape x3, waiting for transfers between devices, step(): t.reshape(-1, *t.shape[2:])  159 us
    dot_general x5, matrix products, layer(): up = jnp.dot(a, w['w_up'], preferred_element_type=jnp.float32)  63.1 us
    dot_general x5, matrix products, layer(): gate = jnp.dot(a, w['w_gate'], preferred_element_type=jnp.float32)  56.3 us
    dot_general x5, matrix products, matmul(): jnp.dot(a, w, preferred_element_type=jnp.float32).astype(jnp.bfloat16)  51.8 us
    reduce_sum x1, blocking collectives, of_a_group(): jnp.sum(g * g)  32.1 us
    unnamed x49, local copies, waits for them, and re-layouts  27.8 us
    unnamed x5, other arithmetic  25 us
  transfers between devices with their start and end apart: 9, of which 8 were waited for; matrix products, arithmetic and copies ran while one was open for 11% of the time, Pallas kernels for 0%

commit v1 on v0

v1 whole, which is shorter than its diff:
```python
import functools
import math

import jax
import jax.numpy as jnp
from jax import lax
from jax.experimental import pallas as pl
from jax.experimental.pallas import tpu as pltpu
from jax.sharding import PartitionSpec as P

MESH = pl.DeviceIdType.MESH
F32, BF16 = jnp.float32, jnp.bfloat16
ANY = pl.BlockSpec(memory_space=pl.ANY)
HELD = pl.BlockSpec(memory_space=pltpu.VMEM)
TILE = 256
BLOCK = 256
UNIT = 16

LAGS = (0, 2, 4, 5, 7)


def schedule(numbers):
    for time in range(2 * numbers + LAGS[-1]):
        if time < 2 * numbers:
            yield 0, time // 2, time % 2
        for step, lag in reversed(list(enumerate(LAGS))):
            number, odd = divmod(time - lag - 1, 2)
            if not odd and 0 <= number < numbers:
                yield from ((step + 1, number, half) for half in (0, 1))


def normed(h):
    wide = h.astype(F32)
    scale = lax.rsqrt(jnp.mean(wide**2, -1, keepdims=True) + 1e-6)
    return (wide * scale).astype(BF16), scale


def sigmoid(x):
    return 0.5 * jnp.tanh(0.5 * x) + 0.5


def mm(a, b):
    return jnp.dot(a, b, preferred_element_type=F32)


def mm_t(a, b):
    return lax.dot_general(a, b, (((1,), (1,)), ((), ())), preferred_element_type=F32)


def token_kernel(layers, x_ref, dy_ref, w_gate, w_up, w_down, *refs):
    lhs, rhs, saved = refs[: 2 * layers], refs[2 * layers : 5 * layers], refs[5 * layers :]
    ff = w_gate.shape[2]
    pieces = [pl.ds(start, TILE) for start in range(0, ff, TILE)]
    h, dh = x_ref[...], dy_ref[...]
    states = []
    for l in range(layers):
        last = l + 1 == layers
        a, scale = normed(h)
        lhs[2 * l][...] = a.T
        states.append((h, scale))
        if last:
            lhs[2 * l + 1][...] = dh.T
        total = back_gate = back_up = None
        for piece in pieces:
            gate, up = mm(a, w_gate[l, :, piece]), mm(a, w_up[l, :, piece])
            s = sigmoid(gate)
            silu = gate * s
            act = (silu * up).astype(BF16)
            rhs[3 * l + 2][:, piece] = act
            slope = up * (s + silu * (1.0 - s))
            if last:
                dact = mm_t(dh, w_down[l, piece, :]).astype(BF16).astype(F32)
                dup, dgate = (dact * silu).astype(BF16), (dact * slope).astype(BF16)
                rhs[3 * l][:, piece], rhs[3 * l + 1][:, piece] = dgate, dup
                p, q = mm_t(dgate, w_gate[l, :, piece]), mm_t(dup, w_up[l, :, piece])
                back_gate = p if back_gate is None else back_gate + p
                back_up = q if back_up is None else back_up + q
            else:
                saved[2 * l][:, piece], saved[2 * l + 1][:, piece] = silu, slope
                p = mm(act, w_down[l, piece, :])
                total = p if total is None else total + p
        if not last:
            h = h + total.astype(BF16)
    for l in reversed(range(layers)):
        if l + 1 < layers:
            lhs[2 * l + 1][...] = dh.T
            back_gate = back_up = None
            for piece in pieces:
                dact = mm_t(dh, w_down[l, piece, :]).astype(BF16).astype(F32)
                dup, dgate = (dact * saved[2 * l][:, piece]).astype(BF16), (dact * saved[2 * l + 1][:, piece]).astype(BF16)
                rhs[3 * l][:, piece], rhs[3 * l + 1][:, piece] = dgate, dup
                if l:
                    p, q = mm_t(dgate, w_gate[l, :, piece]), mm_t(dup, w_up[l, :, piece])
                    back_gate = p if back_gate is None else back_gate + p
                    back_up = q if back_up is None else back_up + q
        if l:
            h, scale = states[l]
            da = (back_gate.astype(BF16) + back_up.astype(BF16)).astype(F32)
            wide = h.astype(F32)
            along = jnp.mean(da * wide, -1, keepdims=True)
            dh = dh + (da * scale - wide * (scale * scale * scale * along)).astype(BF16)


def token_phase(x, dy, ws):
    layers, d, ff = ws[0].shape
    tokens = x.shape[0]
    block = min(BLOCK, tokens)
    whole = [pl.BlockSpec(w.shape, lambda i: (0, 0, 0), pipeline_mode=pl.Buffered(1)) for w in ws]
    rows = lambda width: pl.BlockSpec((block, width), lambda i: (i, 0))
    outs = [jax.ShapeDtypeStruct((d, tokens), BF16)] * (2 * layers) + [jax.ShapeDtypeStruct((tokens, ff), BF16)] * (3 * layers)
    products = 9 if layers == 2 else 8 * layers
    got = pl.pallas_call(
        functools.partial(token_kernel, layers),
        grid=(tokens // block,),
        out_shape=outs,
        in_specs=[rows(d), rows(d), *whole],
        out_specs=[pl.BlockSpec((d, block), lambda i: (0, i))] * (2 * layers) + [rows(ff)] * (3 * layers),
        scratch_shapes=[pltpu.VMEM((block, ff), F32)] * (2 * (layers - 1)),
        compiler_params=pltpu.CompilerParams(vmem_limit_bytes=60 * 2**20),
        cost_estimate=pl.CostEstimate(flops=2 * products * tokens * d * ff, bytes_accessed=2 * 6 * tokens * ff, transcendentals=0),
    )(x, dy, *ws)
    return got[: 2 * layers], got[2 * layers :]


def write_kernel(*refs):
    sources, targets, sem = refs[:9], refs[9:18], refs[18]
    copies = [
        pltpu.make_async_copy(source.at[l], target.at[l], sem.at[i, l])
        for i, (source, target) in enumerate(zip(sources, targets)) for l in range(source.shape[0])
    ]
    for copy in copies:
        copy.start()
    for copy in copies:
        copy.wait()


class Spot:
    def __init__(self, side):
        self.side = side
        me = lax.axis_index("dp")
        self.me, self.at = me, (me // side, me % side)

    def along(self, axis, by):
        return (self.at[axis] + by) % self.side

    def device(self, axis, by):
        x, y = (self.along(a, by) if a == axis else self.at[a] for a in (0, 1))
        return {"dp": x * self.side + y}


def kernel(side, layers, kinds, count, *refs):
    refs = list(refs)
    take = lambda k: [refs.pop(0) for _ in range(k)]
    lhs_in = take(2 * layers)
    rhs_in = take(3 * layers)
    w_in, m_in, v_in = take(3), take(3), take(3)
    terms = take(3)
    m, v = take(3), take(3)
    lhs, rhs = take(2)
    far1, near1, far2, near2, own = (take(3) for _ in range(5))
    grad, w, new = (take(3) for _ in range(3))
    squares = take(1)[0]
    lhs_sem, rhs_sem, io_sem, ssem, rsem, ex_ssem, ex_rsem, ag_ssem, ag_rsem = take(9)
    assert not refs

    spot = Spot(side)
    half_ring = side // 2
    order = [(kind, layer) for layer in reversed(range(layers)) for kind in (0, 1, 2)]

    loads = []
    lhs_loads = {}
    for layer in reversed(range(layers)):
        for which in (0, 1):
            i = 2 * layer + which
            lhs_loads[i] = pltpu.make_async_copy(lhs_in[i], lhs.at[i], lhs_sem.at[i])

    tiles = rhs_in[0].shape[1] // TILE

    def rhs_load(number, tile):
        kind, layer = order[number]
        slot = (number * tiles + tile) % 2
        columns = pl.ds(pl.multiple_of(tile * TILE, TILE), TILE)
        return pltpu.make_async_copy(rhs_in[3 * layer + kind].at[:, columns], rhs.at[slot], rhs_sem.at[slot])

    lhs_loads[2 * (layers - 1)].start()
    rhs_load(0, 0).start()
    for i, load in lhs_loads.items():
        if i != 2 * (layers - 1):
            load.start()
    for kind in range(3):
        rows = kinds[kind][0]
        mine = pl.ds(pl.multiple_of(spot.me * rows, UNIT), rows)
        loads.append(pltpu.make_async_copy(w_in[kind].at[:, mine, :], w[kind], io_sem.at[kind]))
        loads.append(pltpu.make_async_copy(m_in[kind], m[kind], io_sem.at[3 + kind]))
        loads.append(pltpu.make_async_copy(v_in[kind], v[kind], io_sem.at[6 + kind]))
    for load in loads:
        load.start()

    barrier = pltpu.get_barrier_semaphore()
    for axis in (0, 1):
        for by in range(1, side):
            pl.semaphore_signal(barrier, inc=1, device_id=spot.device(axis, by), device_id_type=MESH)
    pl.semaphore_wait(barrier, 2 * (side - 1))

    sent = []

    def send(src, dst, sems, index, device):
        copy = pltpu.make_async_remote_copy(
            src_ref=src, dst_ref=dst, send_sem=sems[0].at[index], recv_sem=sems[1].at[index],
            device_id=device, device_id_type=MESH)
        copy.start()
        sent.append(copy)
        return copy

    ready = set()
    parts = [(0, -(-tiles // 2)), (-(-tiles // 2), tiles)]

    def compute(number, part):
        kind, layer = order[number]
        i = 2 * layer + (kind == 2)
        if i not in ready:
            ready.add(i)
            lhs_loads[i].wait()
        term = terms[kind].at[layer]
        rows, columns = kinds[kind]

        def body(tile, carry):
            slot = (number * tiles + tile) % 2
            rhs_load(number, tile).wait()

            @pl.when(tile + 1 < tiles)
            def _():
                rhs_load(number, tile + 1).start()

            if number + 1 < len(order):
                @pl.when(tile + 1 == tiles)
                def _():
                    rhs_load(number + 1, 0).start()

            product = jnp.dot(lhs[i], rhs[slot], preferred_element_type=F32).astype(BF16)
            if kind < 2:
                here = pl.ds(pl.multiple_of(tile * TILE, TILE), TILE)
                term[:, :, :, here] = product.reshape(side, side, rows, TILE)
            else:
                turned = product.T
                for unit in range(TILE // UNIT):
                    place = tile * (TILE // UNIT) + unit
                    block, row = place // (rows // UNIT), place % (rows // UNIT)
                    term[block // side, block % side, pl.ds(pl.multiple_of(row * UNIT, UNIT), UNIT), :] = (
                        turned[unit * UNIT : (unit + 1) * UNIT])
            return carry

        lax.fori_loop(*parts[part], body, 0)

    class Sum:
        def __init__(self, number, half):
            self.kind, self.layer = order[number]
            self.rows, columns = kinds[self.kind]
            self.width = columns // 2
            self.columns = pl.ds(half * self.width, self.width)
            self.first, self.second, self.half = half, 1 - half, half
            self.term = terms[self.kind].at[self.layer]
            self.base = 8 * (2 * number + half)
            cut = UNIT * (self.rows // UNIT // 2 + (number + half) % 2 * (self.rows // UNIT % 2))
            self.cuts = (pl.ds(0, cut), pl.ds(cut, self.rows - cut))
            b = (self.layer, half)
            self.far1, self.near1, self.far2, self.near2, self.own = (r[self.kind].at[b] for r in (far1, near1, far2, near2, own))
            self.copies = {}

        def block(self, first, second):
            return (first, second) if self.half == 0 else (second, first)

        def go(self, event, way, src, dst, axis):
            sems = (ssem, rsem)
            self.copies[event, way] = send(src, dst, sems, self.base + 2 * event + way, spot.device(axis, 1 - 2 * way))

        def arrived(self, event):
            for way in (0, 1):
                self.copies[event, way].wait_recv()

        def each(self, work):
            def body(unit, carry):
                work(pl.ds(pl.multiple_of(unit * UNIT, UNIT), UNIT))
                return carry
            lax.fori_loop(0, self.rows // UNIT, body, 0)

        def step1(self):
            away = spot.along(self.first, half_ring)
            for way in (0, 1):
                some = pl.ds(way * half_ring, half_ring)
                src = self.term.at[self.block(away, some) + (slice(None), self.columns)]
                self.go(0, way, src, self.far1.at[way], self.first)

        def step2(self):
            self.arrived(0)
            for way in (0, 1):
                to = spot.along(self.first, 1 - 2 * way)

                def work(rows):
                    for j in range(half_ring):
                        at = self.block(to, way * half_ring + j) + (rows, self.columns)
                        total = self.term[at].astype(F32) + self.far1[way, j, rows, :].astype(F32)
                        self.term[at] = total.astype(BF16)

                self.each(work)
                src = self.term.at[self.block(to, slice(None)) + (slice(None), self.columns)]
                self.go(1, way, src, self.near1.at[way], self.first)

        def step3(self):
            self.arrived(1)
            me = spot.at[self.first]

            def total(second, rows):
                at = self.block(me, second) + (rows, self.columns)
                return (self.term[at].astype(F32) + self.near1[0, second, rows, :].astype(F32)) + self.near1[1, second, rows, :].astype(F32)

            def work(rows):
                for by in range(1, side):
                    second = spot.along(self.second, by)
                    self.term[self.block(me, second) + (rows, self.columns)] = total(second, rows).astype(BF16)
                self.own[rows, :] = total(spot.at[self.second], rows)

            self.each(work)
            away = spot.along(self.second, half_ring)
            for way in (0, 1):
                src = self.term.at[self.block(me, away) + (self.cuts[way], self.columns)]
                self.go(2, way, src, self.far2.at[self.cuts[way]], self.second)

        def step4(self):
            self.arrived(2)
            me = spot.at[self.first]
            for way in (0, 1):
                to = spot.along(self.second, 1 - 2 * way)
                at = self.block(me, to) + (self.cuts[way], self.columns)
                self.term[at] = (self.term[at].astype(F32) + self.far2[self.cuts[way]].astype(F32)).astype(BF16)
                src = self.term.at[self.block(me, to) + (slice(None), self.columns)]
                self.go(3, way, src, self.near2.at[way], self.second)

        def step5(self):
            self.arrived(3)

            def work(rows):
                total = (self.own[rows, :] + self.near2[0, rows, :].astype(F32)) + self.near2[1, rows, :].astype(F32)
                grad[self.kind][self.layer, rows, self.columns] = total.astype(BF16)

            self.each(work)

    sums = {(number, half): Sum(number, half) for number in range(len(order)) for half in (0, 1)}
    for what, number, which in schedule(len(order)):
        if what == 0:
            compute(number, which)
        else:
            getattr(sums[number, which], f"step{what}")()

    for copy in sent:
        copy.wait_send()
    sent.clear()

    part = jnp.zeros((8, 128), F32)
    for kind in range(3):
        rows, columns = kinds[kind]
        for layer in range(layers):
            def body(unit, part):
                g = grad[kind][layer, pl.ds(pl.multiple_of(unit * UNIT, UNIT), UNIT), :].astype(F32)
                g = g * g
                for i in range(UNIT // 8):
                    for j in range(columns // 128):
                        part = part + g[8 * i : 8 * i + 8, 128 * j : 128 * j + 128]
                return part
            part = lax.fori_loop(0, rows // UNIT, body, part)
    for axis in (0, 1):
        mine = spot.at[axis]
        squares[axis, mine] = part
        for by in range(1, side):
            copy = pltpu.make_async_remote_copy(
                src_ref=squares.at[axis, mine], dst_ref=squares.at[axis, mine], send_sem=ex_ssem.at[axis, by], recv_sem=ex_rsem.at[axis, mine],
                device_id=spot.device(axis, by), device_id_type=MESH)
            copy.start()
            sent.append(copy)
        for by in range(1, side):
            other = spot.along(axis, by)
            pltpu.make_async_remote_copy(
                src_ref=squares.at[axis, other], dst_ref=squares.at[axis, other], send_sem=ex_ssem.at[axis, by], recv_sem=ex_rsem.at[axis, other],
                device_id=spot.device(axis, by), device_id_type=MESH).wait_recv()
        part = squares[axis, 0]
        for i in range(1, side):
            part = part + squares[axis, i]
    total = jnp.sum(jnp.sum(part, 0, keepdims=True), 1, keepdims=True)
    factor = jnp.minimum(1.0, 0.5 * lax.rsqrt(total / count + 1e-30))

    for load in loads:
        load.wait()
    for kind in range(3):
        rows, columns = kinds[kind]

        def body(unit, carry):
            layer, unit = unit // (rows // UNIT), unit % (rows // UNIT)
            at = (layer, pl.ds(pl.multiple_of(unit * UNIT, UNIT), UNIT), slice(None))
            g = grad[kind][at].astype(F32) * factor
            m1 = 0.9 * m[kind][at] + 0.1 * g
            v1 = 0.95 * v[kind][at] + 0.05 * g * g
            wide = w[kind][at].astype(F32)
            m[kind][at], v[kind][at] = m1, v1
            fresh = (wide - 0.02 * (m1 * lax.rsqrt(v1 + 1e-8) + 0.1 * wide)).astype(BF16)
            new[kind][at] = fresh
            terms[kind][(layer, *spot.at, *at[1:])] = fresh
            return carry

        lax.fori_loop(0, layers * (rows // UNIT), body, 0)

    class Gather:
        def __init__(self, half, kind):
            self.half, self.kind = half, kind
            self.rows, columns = kinds[kind]
            self.columns = pl.ds(half * (columns // 2), columns // 2)
            self.first, self.second = half, 1 - half
            self.base = 20 * (3 * half + kind)

        def place(self, by_first, by_second, some=slice(None)):
            a, b = spot.along(self.first, by_first), spot.along(self.second, by_second)
            x, y = (a, b) if self.half == 0 else (b, a)
            return terms[self.kind].at[some, x, y, :, self.columns]

        def go(self, index, way, axis, at, src=None):
            send(at if src is None else src, at, (ag_ssem, ag_rsem), self.base + index + way, spot.device(axis, 1 - 2 * way))

        def arrived(self, index, way, at):
            pltpu.make_async_remote_copy(
                src_ref=at, dst_ref=at, send_sem=ag_ssem.at[self.base + index + way], recv_sem=ag_rsem.at[self.base + index + way],
                device_id=spot.device(0, 1), device_id_type=MESH).wait_recv()

        def some(self, way):
            return pl.ds(way * (layers // 2), layers // 2)

        def start(self):
            src = new[self.kind].at[:, :, self.columns]
            for way in (0, 1):
                self.go(0, way, self.first, self.place(0, 0), src)
            for way in (0, 1):
                self.go(4, way, self.second, self.place(0, 0), src)

        def first_near(self, way):
            by = 2 * way - 1
            self.arrived(0, way, self.place(by, 0))
            self.go(2, way, self.first, self.place(by, 0, self.some(way)))
            for to in (0, 1):
                self.go(8 + 4 * way, to, self.second, self.place(by, 0))

        def first_far(self):
            for way in (0, 1):
                self.arrived(2, way, self.place(half_ring, 0, self.some(way)))
            for to in (0, 1):
                self.go(16, to, self.second, self.place(half_ring, 0))

        def second_near(self, which):
            by_first = (0, -1, 1, half_ring)[which]
            for way in (0, 1):
                by = 2 * way - 1
                self.arrived(4 + 4 * which, way, self.place(by_first, by))
                self.go(6 + 4 * which, way, self.second, self.place(by_first, by, self.some(way)))

        def second_far(self, which):
            by_first = (0, -1, 1, half_ring)[which]
            for way in (0, 1):
                self.arrived(6 + 4 * which, way, self.place(by_first, half_ring, self.some(way)))

    gathers = [Gather(half, kind) for kind in range(3) for half in (0, 1)]
    for gather in gathers:
        gather.start()
    for way in (0, 1):
        for gather in gathers:
            gather.first_near(way)
    for gather in gathers:
        gather.second_near(0)
    for gather in gathers:
        gather.first_far()
    for which in (1, 2, 3):
        for gather in gathers:
            gather.second_near(which)
    for which in range(4):
        for gather in gathers:
            gather.second_far(which)
    for copy in sent:
        copy.wait_send()


def solution(mesh):
    n = mesh.shape["dp"]
    side = math.isqrt(n)

    def update(lhs, rhs, ws, ms, vs):
        layers = ws[0].shape[0]
        d, tokens = lhs[0].shape
        kinds = tuple((m.shape[1], m.shape[2]) for m in ms)
        count = float(sum(w.size for w in ws))
        scratch = [pltpu.VMEM((2 * layers, d, tokens), BF16), pltpu.VMEM((2, tokens, TILE), BF16)]
        scratch += [pltpu.VMEM((layers, 2, 2, side // 2, r, c // 2), BF16) for r, c in kinds]
        scratch += [pltpu.VMEM((layers, 2, 2, side, r, c // 2), BF16) for r, c in kinds]
        scratch += [pltpu.VMEM((layers, 2, r, c // 2), BF16) for r, c in kinds]
        scratch += [pltpu.VMEM((layers, 2, 2, r, c // 2), BF16) for r, c in kinds]
        scratch += [pltpu.VMEM((layers, 2, r, c // 2), F32) for r, c in kinds]
        for dtype in (BF16, BF16, BF16):
            scratch += [pltpu.VMEM((layers, r, c), dtype) for r, c in kinds]
        scratch += [pltpu.VMEM((2, side, 8, 128), F32)]
        dma = pltpu.SemaphoreType.DMA
        sums, gathers = 8 * 2 * 3 * layers, 20 * 6
        scratch += [dma((2 * layers,)), dma((2,)), dma((9,)), dma((sums,)), dma((sums,)),
                    dma((2, side)), dma((2, side)), dma((gathers,)), dma((gathers,))]
        got = pl.pallas_call(
            functools.partial(kernel, side, layers, kinds, count),
            out_shape=[pltpu.VMEM((layers, side, side, r, c), BF16) for r, c in kinds] + [pltpu.VMEM(m.shape, F32) for m in (*ms, *vs)],
            in_specs=[ANY] * (len(lhs) + len(rhs) + 9),
            out_specs=[HELD] * 9,
            scratch_shapes=scratch,
            compiler_params=pltpu.CompilerParams(collective_id=0, has_side_effects=True, vmem_limit_bytes=40 * 2**20),
        )(*lhs, *rhs, *ws, *ms, *vs)
        out = pl.pallas_call(
            write_kernel,
            out_shape=[jax.ShapeDtypeStruct(t.shape, t.dtype) for t in got],
            in_specs=[HELD] * 9,
            out_specs=[ANY] * 9,
            scratch_shapes=[dma((9, layers))],
            compiler_params=pltpu.CompilerParams(vmem_limit_bytes=4 * 2**20),
        )(*got)
        return [t.reshape(w.shape) for t, w in zip(out, (*ws, *ms, *vs))]

    def step(x, dy, *arrays):
        ws, ms, vs = (arrays[i : i + 3] for i in (0, 3, 6))
        lhs, rhs = token_phase(x[0], dy[0], ws)
        return tuple(update(lhs, rhs, ws, ms, vs))

    data, whole, rows = P(("rep", "dp")), P(), P(None, "dp")
    return jax.shard_map(
        step, mesh=mesh,
        in_specs=(data, data, whole, whole, whole) + (rows,) * 6,
        out_specs=(P("rep"),) * 3 + (P("rep", "dp"),) * 6,
        check_vma=False,
    )
```

time: 840 us -> 301 us (0.36)
  the two profiles are of different devices: /device:TPU:97 before, /device:TPU:96 now
where the time goes in v1:
time: 301 us; the launch traced here: 300 us
  Pallas kernels  299 us (99%)
    pallas_call x1, Pallas kernels, update(): pl.pallas_call(functools.partial(kernel, side, layers, kinds, count), out...  209 us
    pallas_call x1, Pallas kernels, token_phase(): pl.pallas_call(functools.partial(token_kernel, layers), grid=(tokens // b...  83.1 us
    pallas_call x1, Pallas kernels, update(): pl.pallas_call(write_kernel, out_shape=[jax.ShapeDtypeStruct(t.shape, t.d...  7.16 us

profile of v1, /device:TPU:96, one launch (start us, length us, event | category | flops | bytes accessed | tf_op | source)
XLA Modules:
  0.0 299.6 jit_solution(10869704830381121960)
XLA Ops:
  0.6 83.1 %shard_map.178 = (bf16[768,2048]{1,0:T(8,128)(2,1)}, bf16[768,2048]{1,0:T(8,128)(2,1)}, bf16[768,2048]{1,0:T(8,128)(2,1)}, bf16[768,2048]{1,0:T(8,128)(2,1)}, bf...) custom-call(bf16[2048,768]{1,0:T(8,128)(2,1)} %bitcast.8, ...), custom_call_target="tpu_custom_call" | custom-call | flops 50734301184 | bytes 44040192 | tf_op jit(solution)/shard_map/pallas_call | solution.py:112
  83.7 208.5 %shard_map.179 = (bf16[2,4,4,48,1792]{4,3,2,1,0:T(8,128)(2,1)S(1)}, bf16[2,4,4,48,1792]{4,3,2,1,0:T(8,128)(2,1)S(1)}, bf16[2,4,4,112,768]{4,3,2,1,0:T(8,128)(2,1...) custom-call(bf16[768,2048]{1,0:T(8,128)(2,1)} %get-tuple-element.37., ...), custom_call_target="tpu_custom_call" | custom-call | tf_op jit(solution)/shard_map/pallas_call | solution.py:509
  292.2 7.2 %shard_map.180 = (bf16[2,4,4,48,1792]{4,3,2,1,0:T(8,128)(2,1)}, bf16[2,4,4,48,1792]{4,3,2,1,0:T(8,128)(2,1)}, bf16[2,4,4,112,768]{4,3,2,1,0:T(8,128)(2,1)}, f32[...) custom-call(bf16[2,4,4,48,1792]{4,3,2,1,0:T(8,128)(2,1)S(1)} %get-tu, ...), custom_call_target="tpu_custom_call" | custom-call | tf_op jit(solution)/shard_map/pallas_call | solution.py:517

commit v2 on v1

--- a/solution.py
+++ b/solution.py
@@ -16,17 +16,50 @@
 BLOCK = 256
 UNIT = 16
 
-LAGS = (0, 2, 4, 5, 7)
-
-
-def schedule(numbers):
-    for time in range(2 * numbers + LAGS[-1]):
-        if time < 2 * numbers:
-            yield 0, time // 2, time % 2
-        for step, lag in reversed(list(enumerate(LAGS))):
-            number, odd = divmod(time - lag - 1, 2)
-            if not odd and 0 <= number < numbers:
-                yield from ((step + 1, number, half) for half in (0, 1))
+ORDER = ((0, 1), (1, 1), (2, 1), (2, 0), (0, 0), (1, 0))
+SEGMENTS = 4
+HALF, PIECE, LATENCY = 3.6, 9.0, 2.3
+WORK, WIRE = (0.1, 0.7, 1.0, 0.3, 0.4), (3.6, 7.2, 0.9, 1.8)
+
+
+def schedule():
+    turn = [i for i in range(1, len(ORDER)) if ORDER[i][1] != ORDER[i - 1][1]][0]
+    products = [(0, number, half) for number in range(len(ORDER)) for half in (0, 1)]
+    products[2 * turn : 2 * turn] = [(6, 0, piece) for piece in range(SEGMENTS)]
+    now, free, due, done = 2.0, [0.0, 0.0], {}, set()
+
+    def may(event):
+        step, number, half = event
+        kind = ORDER[number][0]
+        if step == 1:
+            return all((5, other, i) in done for other in range(number) if ORDER[other][0] == kind for i in (0, 1))
+        return step != 4 or all((3, number, i) in done for i in (0, 1))
+
+    while products or due:
+        can = [event for event in due if may(event)]
+        here = [event for event in can if due[event] <= now]
+        if here:
+            event = min(here)
+        elif products:
+            event = products.pop(0)
+        else:
+            event = min(can, key=lambda event: (due[event], event))
+        step, number, half = event
+        if step == 6:
+            now += PIECE
+        elif step == 0:
+            now += HALF
+            for i in (0, 1):
+                if half == i if ORDER[number][0] < 2 else half:
+                    due[1, number, i] = now
+        else:
+            now = max(now, due.pop(event)) + WORK[step - 1]
+            if step < 5:
+                axis = half if step < 3 else 1 - half
+                free[axis] = max(free[axis], now) + WIRE[step - 1]
+                due[step + 1, number, half] = free[axis] + LATENCY
+        done.add(event)
+        yield event
 
 
 def normed(h):
@@ -47,79 +80,56 @@
     return lax.dot_general(a, b, (((1,), (1,)), ((), ())), preferred_element_type=F32)
 
 
-def token_kernel(layers, x_ref, dy_ref, w_gate, w_up, w_down, *refs):
-    lhs, rhs, saved = refs[: 2 * layers], refs[2 * layers : 5 * layers], refs[5 * layers :]
-    ff = w_gate.shape[2]
-    pieces = [pl.ds(start, TILE) for start in range(0, ff, TILE)]
-    h, dh = x_ref[...], dy_ref[...]
-    states = []
-    for l in range(layers):
-        last = l + 1 == layers
-        a, scale = normed(h)
-        lhs[2 * l][...] = a.T
-        states.append((h, scale))
-        if last:
-            lhs[2 * l + 1][...] = dh.T
-        total = back_gate = back_up = None
-        for piece in pieces:
-            gate, up = mm(a, w_gate[l, :, piece]), mm(a, w_up[l, :, piece])
-            s = sigmoid(gate)
-            silu = gate * s
-            act = (silu * up).astype(BF16)
-            rhs[3 * l + 2][:, piece] = act
-            slope = up * (s + silu * (1.0 - s))
-            if last:
-                dact = mm_t(dh, w_down[l, piece, :]).astype(BF16).astype(F32)
-                dup, dgate = (dact * silu).astype(BF16), (dact * slope).astype(BF16)
-                rhs[3 * l][:, piece], rhs[3 * l + 1][:, piece] = dgate, dup
-                p, q = mm_t(dgate, w_gate[l, :, piece]), mm_t(dup, w_up[l, :, piece])
-                back_gate = p if back_gate is None else back_gate + p
-                back_up = q if back_up is None else back_up + q
-            else:
-                saved[2 * l][:, piece], saved[2 * l + 1][:, piece] = silu, slope
-                p = mm(act, w_down[l, piece, :])
-                total = p if total is None else total + p
-        if not last:
-            h = h + total.astype(BF16)
-    for l in reversed(range(layers)):
-        if l + 1 < layers:
-            lhs[2 * l + 1][...] = dh.T
-            back_gate = back_up = None
-            for piece in pieces:
-                dact = mm_t(dh, w_down[l, piece, :]).astype(BF16).astype(F32)
-                dup, dgate = (dact * saved[2 * l][:, piece]).astype(BF16), (dact * saved[2 * l + 1][:, piece]).astype(BF16)
-                rhs[3 * l][:, piece], rhs[3 * l + 1][:, piece] = dgate, dup
-                if l:
-                    p, q = mm_t(dgate, w_gate[l, :, piece]), mm_t(dup, w_up[l, :, piece])
-                    back_gate = p if back_gate is None else back_gate + p
-                    back_up = q if back_up is None else back_up + q
-        if l:
-            h, scale = states[l]
-            da = (back_gate.astype(BF16) + back_up.astype(BF16)).astype(F32)
-            wide = h.astype(F32)
-            along = jnp.mean(da * wide, -1, keepdims=True)
-            dh = dh + (da * scale - wide * (scale * scale * scale * along)).astype(BF16)
+def token_kernel(x_ref, dy_ref, w_gate, w_up, w_down, a_first, a_last, turned_dy, act_first, dgate, dup, act_last, silu_first, slope_first, h_last):
+    pieces = [pl.ds(start, TILE) for start in range(0, w_gate.shape[2], TILE)]
+    dh = dy_ref[...]
+    turned_dy[...] = dh.T
+    h = x_ref[...]
+    a, _ = normed(h)
+    a_first[...] = a.T
+    total = None
+    for piece in pieces:
+        gate, up = mm(a, w_gate[0, :, piece]), mm(a, w_up[0, :, piece])
+        silu, slope = slopes(gate, up)
+        act = (silu * up).astype(BF16)
+        act_first[:, piece], silu_first[:, piece], slope_first[:, piece] = act, silu, slope
+        p = mm(act, w_down[0, piece, :])
+        total = p if total is None else total + p
+    h = h + total.astype(BF16)
+    h_last[...] = h
+    a, _ = normed(h)
+    a_last[...] = a.T
+    for piece in pieces:
+        gate, up = mm(a, w_gate[1, :, piece]), mm(a, w_up[1, :, piece])
+        silu, slope = slopes(gate, up)
+        act_last[:, piece] = (silu * up).astype(BF16)
+        dact = mm_t(dh, w_down[1, piece, :]).astype(BF16).astype(F32)
+        dgate[:, piece], dup[:, piece] = (dact * slope).astype(BF16), (dact * silu).astype(BF16)
+
+
+def slopes(gate, up):
+    s = sigmoid(gate)
+    silu = gate * s
+    return silu, up * (s + silu * (1.0 - s))
 
 
 def token_phase(x, dy, ws):
-    layers, d, ff = ws[0].shape
+    _, d, ff = ws[0].shape
     tokens = x.shape[0]
     block = min(BLOCK, tokens)
     whole = [pl.BlockSpec(w.shape, lambda i: (0, 0, 0), pipeline_mode=pl.Buffered(1)) for w in ws]
     rows = lambda width: pl.BlockSpec((block, width), lambda i: (i, 0))
-    outs = [jax.ShapeDtypeStruct((d, tokens), BF16)] * (2 * layers) + [jax.ShapeDtypeStruct((tokens, ff), BF16)] * (3 * layers)
-    products = 9 if layers == 2 else 8 * layers
-    got = pl.pallas_call(
-        functools.partial(token_kernel, layers),
+    turned = pl.BlockSpec((d, block), lambda i: (0, i))
+    shape = jax.ShapeDtypeStruct
+    return pl.pallas_call(
+        token_kernel,
         grid=(tokens // block,),
-        out_shape=outs,
+        out_shape=[shape((d, tokens), BF16)] * 3 + [shape((tokens, ff), BF16)] * 4 + [shape((tokens, ff), F32)] * 2 + [shape((tokens, d), BF16)],
         in_specs=[rows(d), rows(d), *whole],
-        out_specs=[pl.BlockSpec((d, block), lambda i: (0, i))] * (2 * layers) + [rows(ff)] * (3 * layers),
-        scratch_shapes=[pltpu.VMEM((block, ff), F32)] * (2 * (layers - 1)),
-        compiler_params=pltpu.CompilerParams(vmem_limit_bytes=60 * 2**20),
-        cost_estimate=pl.CostEstimate(flops=2 * products * tokens * d * ff, bytes_accessed=2 * 6 * tokens * ff, transcendentals=0),
+        out_specs=[turned] * 3 + [rows(ff)] * 6 + [rows(d)],
+        compiler_params=pltpu.CompilerParams(vmem_limit_bytes=64 * 2**20 - 2**16),
+        cost_estimate=pl.CostEstimate(flops=12 * tokens * d * ff, bytes_accessed=24 * tokens * ff, transcendentals=0),
     )(x, dy, *ws)
-    return got[: 2 * layers], got[2 * layers :]
 
 
 def write_kernel(*refs):
@@ -148,45 +158,124 @@
         return {"dp": x * self.side + y}
 
 
-def kernel(side, layers, kinds, count, *refs):
+def kernel(side, kinds, count, *refs):
     refs = list(refs)
     take = lambda k: [refs.pop(0) for _ in range(k)]
-    lhs_in = take(2 * layers)
-    rhs_in = take(3 * layers)
+    a_first, a_last, turned_dy, act_first, dgate_last, dup_last, act_last, silu_in, slope_in, h_in, dy_in = take(11)
     w_in, m_in, v_in = take(3), take(3), take(3)
     terms = take(3)
     m, v = take(3), take(3)
-    lhs, rhs = take(2)
+    dgate_first, dup_first = take(2)
+    lhs, rhs, down = take(3)
+    dgate_buf, dup_buf, silu_buf, slope_buf, h_buf, dy_buf, dgate_new, dup_new = take(8)
     far1, near1, far2, near2, own = (take(3) for _ in range(5))
-    grad, w, new = (take(3) for _ in range(3))
+    grad, w = take(3), take(3)
     squares = take(1)[0]
-    lhs_sem, rhs_sem, io_sem, ssem, rsem, ex_ssem, ex_rsem, ag_ssem, ag_rsem = take(9)
+    lhs_sem, rhs_sem, w_sem, block_sem, io_sem, ssem, rsem, ex_ssem, ex_rsem, ag_ssem, ag_rsem = take(11)
     assert not refs
+    layers = terms[0].shape[0]
+    rhs_in = {(0, 1): dgate_last, (1, 1): dup_last, (2, 1): act_last, (2, 0): act_first, (0, 0): dgate_first, (1, 0): dup_first}
+    order = ORDER
 
     spot = Spot(side)
     half_ring = side // 2
-    order = [(kind, layer) for layer in reversed(range(layers)) for kind in (0, 1, 2)]
+
+    size = h_buf.shape[0]
+    blocks = h_in.shape[0] // size
+    pairs = (
+        ((dgate_last, dgate_buf), (dup_last, dup_buf)),
+        ((h_in, h_buf), (dy_in, dy_buf), (silu_in, silu_buf), (slope_in, slope_buf)),
+        ((dgate_first, dgate_new), (dup_first, dup_new)),
+    )
+
+    def block_loads(stage, block):
+        here = pl.ds(pl.multiple_of(block * size, size), size)
+        return [pltpu.make_async_copy(far.at[here, :], near, block_sem.at[stage, i]) for i, (far, near) in enumerate(pairs[stage])]
+
+    def block_stores(block):
+        here = pl.ds(pl.multiple_of(block * size, size), size)
+        return [pltpu.make_async_copy(near, far.at[here, :], block_sem.at[2, i]) for i, (far, near) in enumerate(pairs[2])]
+
+    def weight_loads(kind):
+        return [
+            pltpu.make_async_copy(w_in[kind].at[1, :, pl.ds(i * width, width)], rhs.at[kind, pl.ds(i * d, d), :], w_sem.at[2 * kind + i])
+            for i in (0, 1)
+        ]
+
+    def back(kind, buf):
+        return sum(mm_t(buf[:, i * width : (i + 1) * width], rhs[kind, i * d : (i + 1) * d, :]) for i in (0, 1)).astype(BF16)
+
+    def tokens_backward(piece):
+        if piece == 0:
+            for kind in (0, 1):
+                for load in weight_loads(kind):
+                    load.wait()
+            load_down.wait()
+
+        def body(block, carry):
+            for load in block_loads(0, block):
+                load.wait()
+            da = (back(0, dgate_buf) + back(1, dup_buf)).astype(F32)
+
+            @pl.when(block + 1 < blocks)
+            def _():
+                for load in block_loads(0, block + 1):
+                    load.start()
+
+            @pl.when(block + 1 == blocks)
+            def _():
+                rhs_load(3, 0).start()
+
+            for load in block_loads(1, block):
+                load.wait()
+            h = h_buf[...]
+            _, scale = normed(h)
+            wide = h.astype(F32)
+            along = jnp.mean(da * wide, -1, keepdims=True)
+            dh = dy_buf[...] + (da * scale - wide * (scale * scale * scale * along)).astype(BF16)
+            lhs[1, :, pl.ds(pl.multiple_of(block * size, size), size)] = dh.T
+
+            @pl.when(block > 0)
+            def _():
+                for store in block_stores(block - 1):
+                    store.wait()
+
+            for start in range(0, 2 * width, TILE):
+                some = pl.ds(start, TILE)
+                dact = mm_t(dh, down[some, :]).astype(BF16).astype(F32)
+                dgate_new[:, some], dup_new[:, some] = (dact * slope_buf[:, some]).astype(BF16), (dact * silu_buf[:, some]).astype(BF16)
+            for store in block_stores(block):
+                store.start()
+
+            @pl.when(block + 1 < blocks)
+            def _():
+                for load in block_loads(1, block + 1):
+                    load.start()
+
+            return carry
+
+        lax.fori_loop(piece * blocks // SEGMENTS, (piece + 1) * blocks // SEGMENTS, body, 0)
+        if piece + 1 == SEGMENTS:
+            for store in block_stores(blocks - 1):
+                store.wait()
 
     loads = []
-    lhs_loads = {}
-    for layer in reversed(range(layers)):
-        for which in (0, 1):
-            i = 2 * layer + which
-            lhs_loads[i] = pltpu.make_async_copy(lhs_in[i], lhs.at[i], lhs_sem.at[i])
-
-    tiles = rhs_in[0].shape[1] // TILE
-
-    def rhs_load(number, tile):
-        kind, layer = order[number]
-        slot = (number * tiles + tile) % 2
-        columns = pl.ds(pl.multiple_of(tile * TILE, TILE), TILE)
-        return pltpu.make_async_copy(rhs_in[3 * layer + kind].at[:, columns], rhs.at[slot], rhs_sem.at[slot])
-
-    lhs_loads[2 * (layers - 1)].start()
+    width = rhs.shape[2]
+    d = lhs.shape[1]
+
+    def rhs_load(number, part):
+        return pltpu.make_async_copy(rhs_in[order[number]].at[:, pl.ds(part * width, width)], rhs.at[part], rhs_sem.at[part])
+
+    load_a_last = pltpu.make_async_copy(a_last, lhs.at[0], lhs_sem.at[0])
+    load_dy = pltpu.make_async_copy(turned_dy, lhs.at[1], lhs_sem.at[1])
+    load_a_first = pltpu.make_async_copy(a_first, lhs.at[0], lhs_sem.at[2])
+    load_down = pltpu.make_async_copy(w_in[2].at[0], down, w_sem.at[4])
+    load_a_last.start()
     rhs_load(0, 0).start()
-    for i, load in lhs_loads.items():
-        if i != 2 * (layers - 1):
-            load.start()
+    load_dy.start()
+    load_down.start()
+    for load in (*block_loads(0, 0), *block_loads(1, 0)):
+        load.start()
     for kind in range(3):
         rows = kinds[kind][0]
         mine = pl.ds(pl.multiple_of(spot.me * rows, UNIT), rows)
@@ -212,45 +301,35 @@
         sent.append(copy)
         return copy
 
-    ready = set()
-    parts = [(0, -(-tiles // 2)), (-(-tiles // 2), tiles)]
-
     def compute(number, part):
         kind, layer = order[number]
-        i = 2 * layer + (kind == 2)
-        if i not in ready:
-            ready.add(i)
-            lhs_loads[i].wait()
+        which = kind // 2
         term = terms[kind].at[layer]
         rows, columns = kinds[kind]
-
-        def body(tile, carry):
-            slot = (number * tiles + tile) % 2
-            rhs_load(number, tile).wait()
-
-            @pl.when(tile + 1 < tiles)
-            def _():
-                rhs_load(number, tile + 1).start()
-
-            if number + 1 < len(order):
-                @pl.when(tile + 1 == tiles)
-                def _():
-                    rhs_load(number + 1, 0).start()
-
-            product = jnp.dot(lhs[i], rhs[slot], preferred_element_type=F32).astype(BF16)
+        if part == 0 and (number == 0 or number == 2 or number == 4):
+            {0: load_a_last, 2: load_dy, 4: load_a_first}[number].wait()
+        rhs_load(number, part).wait()
+        if part == 0:
+            rhs_load(number, 1).start()
+        elif number + 1 < len(order) and number != 2:
+            rhs_load(number + 1, 0).start()
+        deep = d // 2
+
+        def body(half, carry):
+            some = pl.ds(pl.multiple_of(half * deep, deep), deep)
+            product = jnp.dot(lhs[which, some, :], rhs[part], preferred_element_type=F32).astype(BF16)
             if kind < 2:
-                here = pl.ds(pl.multiple_of(tile * TILE, TILE), TILE)
-                term[:, :, :, here] = product.reshape(side, side, rows, TILE)
+                term[pl.ds(half * half_ring, half_ring), :, :, pl.ds(part * width, width)] = product.reshape(half_ring, side, rows, width)
             else:
-                turned = product.T
-                for unit in range(TILE // UNIT):
-                    place = tile * (TILE // UNIT) + unit
-                    block, row = place // (rows // UNIT), place % (rows // UNIT)
-                    term[block // side, block % side, pl.ds(pl.multiple_of(row * UNIT, UNIT), UNIT), :] = (
-                        turned[unit * UNIT : (unit + 1) * UNIT])
+                term[pl.ds(part * half_ring, half_ring), :, :, some] = product.T.reshape(half_ring, side, rows, deep)
             return carry
 
-        lax.fori_loop(*parts[part], body, 0)
+        lax.fori_loop(0, 2, body, 0)
+        if number == 1 and part:
+            load_a_first.start()
+        if number == 2:
+            for load in weight_loads(part):
+                load.start()
 
     class Sum:
         def __init__(self, number, half):
@@ -263,8 +342,8 @@
             self.base = 8 * (2 * number + half)
             cut = UNIT * (self.rows // UNIT // 2 + (number + half) % 2 * (self.rows // UNIT % 2))
             self.cuts = (pl.ds(0, cut), pl.ds(cut, self.rows - cut))
-            b = (self.layer, half)
-            self.far1, self.near1, self.far2, self.near2, self.own = (r[self.kind].at[b] for r in (far1, near1, far2, near2, own))
+            self.far1, self.near1 = far1[self.kind].at[half], near1[self.kind].at[half]
+            self.far2, self.near2, self.own = (r[self.kind].at[self.layer, half] for r in (far2, near2, own))
             self.copies = {}
 
         def block(self, first, second):
@@ -346,9 +425,11 @@
             self.each(work)
 
     sums = {(number, half): Sum(number, half) for number in range(len(order)) for half in (0, 1)}
-    for what, number, which in schedule(len(order)):
+    for what, number, which in schedule():
         if what == 0:
             compute(number, which)
+        elif what == 6:
+            tokens_backward(which)
         else:
             getattr(sums[number, which], f"step{what}")()
 
@@ -363,9 +444,10 @@
             def body(unit, part):
                 g = grad[kind][layer, pl.ds(pl.multiple_of(unit * UNIT, UNIT), UNIT), :].astype(F32)
                 g = g * g
-                for i in range(UNIT // 8):
-                    for j in range(columns // 128):
-                        part = part + g[8 * i : 8 * i + 8, 128 * j : 128 * j + 128]
+                tiles = [g[8 * i : 8 * i + 8, 128 * j : 128 * j + 128] for i in range(UNIT // 8) for j in range(columns // 128)]
+                while len(tiles) > 1:
+                    tiles = [sum(tiles[i + 1 : i + 2], tiles[i]) for i in range(0, len(tiles), 2)]
+                part = part + tiles[0]
                 return part
             part = lax.fori_loop(0, rows // UNIT, body, part)
     for axis in (0, 1):
@@ -402,11 +484,10 @@
             wide = w[kind][at].astype(F32)
             m[kind][at], v[kind][at] = m1, v1
             fresh = (wide - 0.02 * (m1 * lax.rsqrt(v1 + 1e-8) + 0.1 * wide)).astype(BF16)
-            new[kind][at] = fresh
             terms[kind][(layer, *spot.at, *at[1:])] = fresh
             return carry
 
-        lax.fori_loop(0, layers * (rows // UNIT), body, 0)
+        lax.fori_loop(0, layers * (rows // UNIT), body, 0, unroll=2)
 
     class Gather:
         def __init__(self, half, kind):
@@ -421,8 +502,8 @@
             x, y = (a, b) if self.half == 0 else (b, a)
             return terms[self.kind].at[some, x, y, :, self.columns]
 
-        def go(self, index, way, axis, at, src=None):
-            send(at if src is None else src, at, (ag_ssem, ag_rsem), self.base + index + way, spot.device(axis, 1 - 2 * way))
+        def go(self, index, way, axis, at):
+            send(at, at, (ag_ssem, ag_rsem), self.base + index + way, spot.device(axis, 1 - 2 * way))
 
         def arrived(self, index, way, at):
             pltpu.make_async_remote_copy(
@@ -433,11 +514,9 @@
             return pl.ds(way * (layers // 2), layers // 2)
 
         def start(self):
-            src = new[self.kind].at[:, :, self.columns]
-            for way in (0, 1):
-                self.go(0, way, self.first, self.place(0, 0), src)
-            for way in (0, 1):
-                self.go(4, way, self.second, self.place(0, 0), src)
+            for index, axis in ((0, self.first), (4, self.second)):
+                for way in (0, 1):
+                    self.go(index, way, axis, self.place(0, 0))
 
         def first_near(self, way):
             by = 2 * way - 1
@@ -488,32 +567,35 @@
     n = mesh.shape["dp"]
     side = math.isqrt(n)
 
-    def update(lhs, rhs, ws, ms, vs):
-        layers = ws[0].shape[0]
-        d, tokens = lhs[0].shape
+    def update(products, dy, ws, ms, vs):
+        layers, d, ff = ws[0].shape
+        tokens = dy.shape[0]
+        block = min(BLOCK, tokens // SEGMENTS)
         kinds = tuple((m.shape[1], m.shape[2]) for m in ms)
         count = float(sum(w.size for w in ws))
-        scratch = [pltpu.VMEM((2 * layers, d, tokens), BF16), pltpu.VMEM((2, tokens, TILE), BF16)]
-        scratch += [pltpu.VMEM((layers, 2, 2, side // 2, r, c // 2), BF16) for r, c in kinds]
-        scratch += [pltpu.VMEM((layers, 2, 2, side, r, c // 2), BF16) for r, c in kinds]
-        scratch += [pltpu.VMEM((layers, 2, r, c // 2), BF16) for r, c in kinds]
-        scratch += [pltpu.VMEM((layers, 2, 2, r, c // 2), BF16) for r, c in kinds]
-        scratch += [pltpu.VMEM((layers, 2, r, c // 2), F32) for r, c in kinds]
-        for dtype in (BF16, BF16, BF16):
-            scratch += [pltpu.VMEM((layers, r, c), dtype) for r, c in kinds]
-        scratch += [pltpu.VMEM((2, side, 8, 128), F32)]
-        dma = pltpu.SemaphoreType.DMA
+        vmem, dma = pltpu.VMEM, pltpu.SemaphoreType.DMA
+        scratch = [vmem((2, d, tokens), BF16), vmem((2, max(tokens, 2 * d), ff // 2), BF16), vmem((ff, d), BF16)]
+        scratch += [vmem((block, ff), BF16)] * 2 + [vmem((block, ff), F32)] * 2 + [vmem((block, d), BF16)] * 2 + [vmem((block, ff), BF16)] * 2
+        scratch += [vmem((2, 2, side // 2, r, c // 2), BF16) for r, c in kinds]
+        scratch += [vmem((2, 2, side, r, c // 2), BF16) for r, c in kinds]
+        scratch += [vmem((layers, 2, r, c // 2), BF16) for r, c in kinds]
+        scratch += [vmem((layers, 2, 2, r, c // 2), BF16) for r, c in kinds]
+        scratch += [vmem((layers, 2, r, c // 2), F32) for r, c in kinds]
+        for _ in range(2):
+            scratch += [vmem((layers, r, c), BF16) for r, c in kinds]
+        scratch += [vmem((2, side, 8, 128), F32)]
         sums, gathers = 8 * 2 * 3 * layers, 20 * 6
-        scratch += [dma((2 * layers,)), dma((2,)), dma((9,)), dma((sums,)), dma((sums,)),
+        scratch += [dma((3,)), dma((2,)), dma((5,)), dma((3, 4)), dma((9,)), dma((sums,)), dma((sums,)),
                     dma((2, side)), dma((2, side)), dma((gathers,)), dma((gathers,))]
         got = pl.pallas_call(
-            functools.partial(kernel, side, layers, kinds, count),
-            out_shape=[pltpu.VMEM((layers, side, side, r, c), BF16) for r, c in kinds] + [pltpu.VMEM(m.shape, F32) for m in (*ms, *vs)],
-            in_specs=[ANY] * (len(lhs) + len(rhs) + 9),
-            out_specs=[HELD] * 9,
+            functools.partial(kernel, side, kinds, count),
+            out_shape=[vmem((layers, side, side, r, c), BF16) for r, c in kinds] + [vmem(m.shape, F32) for m in (*ms, *vs)]
+            + [jax.ShapeDtypeStruct((tokens, ff), BF16)] * 2,
+            in_specs=[ANY] * 20,
+            out_specs=[HELD] * 9 + [ANY] * 2,
             scratch_shapes=scratch,
-            compiler_params=pltpu.CompilerParams(collective_id=0, has_side_effects=True, vmem_limit_bytes=40 * 2**20),
-        )(*lhs, *rhs, *ws, *ms, *vs)
+            compiler_params=pltpu.CompilerParams(collective_id=0, has_side_effects=True, vmem_limit_bytes=42 * 2**20),
+        )(*products, dy, *ws, *ms, *vs)[:9]
         out = pl.pallas_call(
             write_kernel,
             out_shape=[jax.ShapeDtypeStruct(t.shape, t.dtype) for t in got],
@@ -526,8 +608,7 @@
 
     def step(x, dy, *arrays):
         ws, ms, vs = (arrays[i : i + 3] for i in (0, 3, 6))
-        lhs, rhs = token_phase(x[0], dy[0], ws)
-        return tuple(update(lhs, rhs, ws, ms, vs))
+        return tuple(update(token_phase(x[0], dy[0], ws), dy[0], ws, ms, vs))
 
     data, whole, rows = P(("rep", "dp")), P(), P(None, "dp")
     return jax.shard_map(

time: 301 us -> 290 us (0.963)
  the two profiles are of different devices: /device:TPU:96 before, /device:TPU:97 now
where the time goes in v2:
time: 290 us; the launch traced here: 285 us
  Pallas kernels  284 us (98%)
    pallas_call x1, Pallas kernels, update(): pl.pallas_call(functools.partial(kernel, side, kinds, count), out_shape=[...  221 us
    pallas_call x1, Pallas kernels, token_phase(): pl.pallas_call(token_kernel, grid=(tokens // block,), out_shape=[shape((d...  56.8 us
    pallas_call x1, Pallas kernels, update(): pl.pallas_call(write_kernel, out_shape=[jax.ShapeDtypeStruct(t.shape, t.d...  7.16 us

profile of v2, /device:TPU:97, one launch (start us, length us, event | category | flops | bytes accessed | tf_op | source)
XLA Modules:
  0.0 285.3 jit_solution(15567914583836284485)
XLA Ops:
  0.6 56.8 %shard_map.178 = (bf16[768,2048]{1,0:T(8,128)(2,1)}, bf16[768,2048]{1,0:T(8,128)(2,1)}, bf16[768,2048]{1,0:T(8,128)(2,1)}, bf16[2048,1792]{1,0:T(8,128)(2,1)}, b...) custom-call(bf16[2048,768]{1,0:T(8,128)(2,1)} %bitcast.10, ...), custom_call_target="tpu_custom_call" | custom-call | flops 33822867456 | bytes 88080384 | tf_op jit(solution)/shard_map/pallas_call | solution.py:124
  57.4 220.5 %shard_map.179 = (bf16[2,4,4,48,1792]{4,3,2,1,0:T(8,128)(2,1)S(1)}, bf16[2,4,4,48,1792]{4,3,2,1,0:T(8,128)(2,1)S(1)}, bf16[2,4,4,112,768]{4,3,2,1,0:T(8,128)(2,1...) custom-call(bf16[768,2048]{1,0:T(8,128)(2,1)} %get-tuple-element.37., ...), custom_call_target="tpu_custom_call" | custom-call | tf_op jit(solution)/shard_map/pallas_call | solution.py:590
  277.9 7.2 %shard_map.180 = (bf16[2,4,4,48,1792]{4,3,2,1,0:T(8,128)(2,1)}, bf16[2,4,4,48,1792]{4,3,2,1,0:T(8,128)(2,1)}, bf16[2,4,4,112,768]{4,3,2,1,0:T(8,128)(2,1)}, f32[...) custom-call(bf16[2,4,4,48,1792]{4,3,2,1,0:T(8,128)(2,1)S(1)} %get-tu, ...), custom_call_target="tpu_custom_call" | custom-call | tf_op jit(solution)/shard_map/pallas_call | solution.py:599
